TPU v7x, 32 devices: a whole 2x2x4 slice. The times are simulated.
32 devices in a mesh: pipe: 4 (over y, core), vocab: 2 (over x), expert: 4 (over z).
Axes of the slice: x: 2, y: 2, z: 4, core: 2. Of those that a mesh axis runs over, the one named last changes fastest.
Arguments:
- token_ids: int32 [192], replicated, may hold values from 0 to 65535
- routes: int32 [192, 2], replicated, may hold values from 0 to 3, all different within a row; in each aligned block of 192 rows (0 to 191, 192 to 383, ...) at most 144 rows name the same one
- gate_weights: float32 [192, 2], replicated, may hold values from 0.2 to 1
- embed_table: bfloat16 [65536, 7168], P(('pipe', 'vocab'), 'expert'), may hold values from -0.59765625 to 0.59765625
- w_gate: bfloat16 [4, 7168, 2048], P('expert', None, ('pipe', 'vocab')), may hold values from -0.5 to 0.5
- w_up: bfloat16 [4, 7168, 2048], P('expert', None, ('pipe', 'vocab')), may hold values from -0.5 to 0.5
- w_down: bfloat16 [4, 2048, 7168], P('expert', ('pipe', 'vocab')), may hold values from -0.125 to 0.125
Outputs:
- logits: bfloat16 [192, 65536], P('expert', ('pipe', 'vocab'))
Inputs may be any that keep to these rules, and one draw needn't show every extreme that they name: `routes`: each row names 2 different experts; over all 192 rows no expert is named more than 144 times, a bound that some block reaches.
All inputs are finite; a program needn't handle non-finite values.
Results may differ from a plain program's by a relative error of at most 0.025.
Values may be sent and summed in bfloat16 or wider, within the bound.
A program may use at most 128 MiB of HBM per device.

v0:
```python
import jax
import jax.numpy as jnp
from jax import lax
from jax.sharding import PartitionSpec as P


def per_device(token_ids, routes, gate_weights, embed_table, w_gate, w_up, w_down):
    vocab_rows, width_cols = embed_table.shape
    tokens, top_count = routes.shape
    experts = lax.axis_size("expert")
    group_size = lax.axis_size(("pipe", "vocab"))
    capacity = group_size * (3 * tokens * top_count // (2 * experts * group_size))
    row_base = lax.axis_index(("pipe", "vocab")) * vocab_rows
    local_ids = token_ids - row_base
    in_shard = (local_ids >= 0) & (local_ids < vocab_rows)
    lookup_rows = jnp.take(embed_table, jnp.clip(local_ids, 0, vocab_rows - 1), axis=0)
    lookup_rows = jnp.where(in_shard[:, None], lookup_rows.astype(jnp.float32), 0.0)
    embedded = lax.psum(lookup_rows.astype(jnp.bfloat16), ("pipe", "vocab"))
    flat_routes = routes.reshape(-1)
    one_hot = (flat_routes[:, None] == jnp.arange(experts, dtype=jnp.int32)[None, :]).astype(
        jnp.int32
    )
    slot_index = jnp.sum((jnp.cumsum(one_hot, axis=0) - one_hot) * one_hot, axis=1)
    slot_dest = flat_routes * capacity + slot_index
    repeated = jnp.repeat(embedded, top_count, axis=0)
    buffer = jnp.zeros((experts * capacity, width_cols), jnp.bfloat16).at[slot_dest].set(repeated)
    buffer = buffer.reshape(experts, capacity, width_cols)
    flat_rows = lax.all_to_all(buffer, "expert", split_axis=0, concat_axis=2, tiled=True)[0]
    gate_proj = jnp.dot(flat_rows, w_gate[0], preferred_element_type=jnp.float32)
    up_proj = jnp.dot(flat_rows, w_up[0], preferred_element_type=jnp.float32)
    hidden = (jax.nn.silu(gate_proj) * up_proj).astype(jnp.bfloat16)
    partial_value = jnp.dot(hidden, w_down[0], preferred_element_type=jnp.float32)[None]
    shared = lax.psum_scatter(
        partial_value.astype(jnp.bfloat16), ("pipe", "vocab"), scatter_dimension=1, tiled=True
    ).astype(jnp.float32)
    shared = lax.all_to_all(
        shared.astype(jnp.bfloat16), "expert", split_axis=2, concat_axis=0, tiled=True
    ).astype(shared.dtype)
    returned = lax.all_gather(
        shared.astype(jnp.bfloat16), ("pipe", "vocab"), axis=1, tiled=True
    ).astype(shared.dtype)
    picked = returned.reshape(experts * capacity, width_cols)[slot_dest].reshape(
        tokens, top_count, width_cols
    )
    moe_out = jnp.sum(picked * gate_weights[:, :, None], axis=1)
    residual = (embedded.astype(jnp.float32) + moe_out).astype(jnp.bfloat16)
    return lax.psum_scatter(
        lax.dot_general(
            residual, embed_table, (((1,), (1,)), ((), ())), preferred_element_type=jnp.float32
        ).astype(jnp.bfloat16),
        "expert",
        scatter_dimension=0,
        tiled=True,
    )


def solution(mesh):
    return jax.shard_map(
        per_device,
        mesh=mesh,
        in_specs=(
            P(),
            P(),
            P(),
            P(("pipe", "vocab"), "expert"),
            P("expert", None, ("pipe", "vocab")),
            P("expert", None, ("pipe", "vocab")),
            P("expert", ("pipe", "vocab"), None),
        ),
        out_specs=P("expert", ("pipe", "vocab")),
        check_vma=False,
    )
```

profile of v0, /device:TPU:0, one launch (start us, length us, event | category | flops | bytes accessed | tf_op | source)
XLA Modules:
  0.0 428.2 jit_solution(8567750402209135640)
XLA Ops:
  6.5 0.7 compare_and_fusion
  7.2 14.9 %gather_fusion = bf16[192,1792]{1,0:T(8,128)(2,1)S(1)} fusion(bf16[8192,1792]{1,0:T(8,128)(2,1)} %param.10, s32[1024]{0:T(1024)S(1)} %pad_clamp_fusion.1), kind=kCustom, calls=%fused_computation | custom fusion | bytes 1377024 | tf_op jit(solution)/shard_map/jit(_take)/gather | solution.py:16
  22.1 1.2 select_convert_fusion
  23.8 1.2 reduce-window.6
  25.9 55.8 %all-reduce.4.cloned.1.call-done = bf16[192,1792]{1,0:T(8,128)(2,1)} async-done(((bf16[192,1792]{1,0:T(8,128)(2,1)}), bf16[192,1792]{1,0:T(8,128)(2,1)}) %all-reduce.4.cloned.1.call-update) | async-done | bytes 688144 | tf_op jit(solution)/shard_map/psum | solution.py:18
  81.6 1.8 broadcast_in_dim.42
  84.0 3.3 scatter_custom_fusion
  87.3 51.2 %all_to_all.33 = bf16[4,144,1792]{2,1,0:T(8,128)(2,1)S(1)} all-to-all(bf16[4,144,1792]{2,1,0:T(8,128)(2,1)S(1)} %bitcast.66), channel_id=1, replica_groups=mesh['pipe'=4,'vocab'=2,'expert'=4] {'expert'}, dimensions={0} | all-to-all | bytes 4128768 | tf_op jit(solution)/shard_map/all_to_all | solution.py:28
  138.5 1.1 copy.41
  139.8 1.8 copy-done
  141.6 0.8 fusion.5
  142.4 6.9 %fusion.1 = bf16[1,144,7168]{2,1,0:T(8,128)(2,1)} fusion(bf16[1,256,7168]{2,1,0:T(8,128)(2,1)} %param.13, bf16[144,7168]{1,0:T(8,128)(2,1)S(1)} %bitcast.63, bf16[1,7168,256]{2,1,0:T(8,128)(2,1)} %param.12, f32[144,256]{1,0:T(8,128)S(1)} %fusion.5), kind=kOutput, calls=%fused_computation.5 | convolution fusion | flops 1058217984 | bytes 11616256 | tf_op jit(solution)/shard_map/dot_general | solution.py:32
  149.2 58.3 %fusion = bf16[24,7168]{1,0:T(8,128)(2,1)S(1)} fusion(bf16[1,144,7168]{2,1,0:T(8,128)(2,1)} %fusion.1), kind=kCustom, calls=%all-reduce-scatter | all-reduce-scatter fusion | flops 1376257 | bytes 2408960
  207.6 1.9 collective-permute-start
  209.6 1.7 collective-permute-start.1
  212.6 4.5 %collective-permute-done = bf16[24,7168]{1,0:T(8,128)(2,1)S(1)} collective-permute-done((bf16[24,7168]{1,0:T(8,128)(2,1)S(1)}, bf16[24,7168]{1,0:T(8,128)(2,1)S(1)}, u32[]{:S(2)}, u32[]{:S(2)}) %collective-permute-start) | collective-permute-done | bytes 344096
  217.0 4.8 %concatenate = bf16[66,7168]{1,0:T(8,128)(2,1)S(1)} concatenate(bf16[18,7168]{1,0:T(8,128)(2,1)S(1)} %collective-permute-done.1, bf16[24,7168]{1,0:T(8,128)(2,1)S(1)} %collective-permute-done, bf16[24,7168]{1,0:T(8,128)(2,1)S(1)} %fusion), dimensions={0} | concatenate | bytes 1892352
  222.0 6.0 %copy.42 = bf16[1,18,7168]{1,0,2:T(2,128)(2,1)} copy(bf16[1,18,7168]{2,1,0:T(8,128)(2,1)S(1)} %dynamic-slice_bitcast_fusion) | data formatting | bytes 516096 | tf_op jit(solution)/shard_map/reduce_scatter | solution.py:33
  228.5 39.8 %reduce.4 = bf16[7168,18]{1,0:T(8,128)(2,1)S(1)} reduce(bf16[7168,1,18]{2,1,0:T(2,128)(2,1)} %bitcast.64, bf16[]{:T(256)} %broadcast.68), dimensions={1}, to_apply=%bitcast.56.reduce_sub_computation | reduce | bytes 516098
  268.3 3.4 reshape.114
  271.7 9.8 %all_to_all.34 = bf16[4,2,16128]{2,1,0:T(2,128)(2,1)S(1)} all-to-all(bf16[4,2,16128]{2,1,0:T(2,128)(2,1)S(1)} %reshape.114), channel_id=1, replica_groups=mesh['pipe'=4,'vocab'=2,'expert'=4] {'expert'}, dimensions={0} | all-to-all | bytes 516096 | tf_op jit(solution)/shard_map/all_to_all | solution.py:36
  281.4 5.2 %reshape.115 = bf16[7168,1,18]{2,1,0:T(2,128)(2,1)} reshape(bf16[4,2,16128]{2,1,0:T(2,128)(2,1)S(1)} %all_to_all.34) | data formatting | bytes 516096
  286.6 7.3 %copy.43 = bf16[1,18,7168]{2,1,0:T(8,128)(2,1)S(1)} copy(bf16[1,18,7168]{1,0,2:T(2,128)(2,1)} %bitcast.65) | data formatting | bytes 516096 | tf_op jit(solution)/shard_map/all_to_all | solution.py:36
  293.9 0.8 all_to_all.28
  295.1 29.7 %all-gather.3.cloned.1.call-done = bf16[4,1,144,1792]{3,0,1,2:T(4,128)(2,1)} async-done(((bf16[4,1,18,1792]{3,0,1,2:T(4,128)(2,1)}), bf16[4,1,144,1792]{3,0,1,2:T(4,128)(2,1)}) %all-gather.3.cloned.1.call-update) | async-done | bytes 2064400 | tf_op jit(solution)/shard_map/all_gather | solution.py:39
  324.8 1.8 copy.45
  326.6 2.4 bitcast_convert_fusion
  329.0 6.1 %gather_fusion.1 = f32[384,1792]{1,0:T(8,128)S(1)} fusion(f32[576,1792]{1,0:T(8,128)} %bitcast_convert_fusion, s32[1024]{0:T(1024)S(1)} %pad_clamp_fusion), kind=kCustom, calls=%fused_computation.1 | custom fusion | bytes 5506560 | tf_op jit(solution)/shard_map/gather | solution.py:42
  335.1 2.8 reshape.75
  337.8 5.9 %multiply_reduce_fusion = f32[192,1792]{1,0:T(8,128)S(1)} fusion(f32[192,2,1792]{2,1,0:T(2,128)} %reshape.75, f32[192,2]{1,0:T(8,128)S(1)} %copy.46), kind=kLoop, calls=%fused_computation.11 | loop fusion | flops 1032192 | bytes 4130304 | tf_op jit(solution)/shard_map/reduce_sum | solution.py:45
  343.8 17.4 %convolution_convert_fusion = bf16[192,8192]{1,0:T(8,128)(2,1)} fusion(bf16[8192,1792]{1,0:T(8,128)(2,1)} %param.10, f32[192,1792]{1,0:T(8,128)S(1)} %multiply_reduce_fusion, bf16[192,1792]{1,0:T(8,128)(2,1)S(1)} %copy-done.1), kind=kOutput, calls=%fused_computation.3 | convolution fusion | flops 5639749632 | bytes 34570240 | tf_op jit(solution)/shard_map/dot_general | solution.py:48
  361.1 60.6 %reduce-scatter.5.cloned.1.call-done = bf16[48,8192]{1,0:T(8,128)(2,1)} async-done(((bf16[192,8192]{1,0:T(8,128)(2,1)}), bf16[48,8192]{1,0:T(8,128)(2,1)}) %reduce-scatter.5.cloned.1.call-update) | async-done | bytes 786448 | tf_op jit(solution)/shard_map/reduce_scatter | solution.py:47
  (37 shorter events, 3.8 us)
Async XLA Ops:
  6.5 75.1 %all-reduce.4.cloned.1.call-start = ((), (), s32[]{:S(2)}) async-start(), calls=%async_computation.3 | async-start | bytes 1376256 | tf_op jit(solution)/shard_map/psum | solution.py:18
  22.1 1.3 copy-start.2
  23.3 301.5 %all-gather.3.cloned.1.call-start = ((), (), s32[]{:S(2)}) async-start(), calls=%async_computation.5 | async-start | bytes 2322432 | tf_op jit(solution)/shard_map/all_gather | solution.py:39
  139.5 2.0 copy-start
  149.2 62.1 %copy-start.4 = (u32[32]{0:T(128)S(1)}, u32[32]{0:T(128)}, u32[]{:S(2)}) copy-start(u32[32]{0:T(128)} %constant.54) | copy-start | bytes 388
  207.6 9.5 %collective-permute-start = (bf16[24,7168]{1,0:T(8,128)(2,1)S(1)}, bf16[24,7168]{1,0:T(8,128)(2,1)S(1)}, u32[]{:S(2)}, u32[]{:S(2)}) collective-permute-start(bf16[24,7168]{1,0:T(8,128)(2,1)S(1)} %fusion), channel_id=1, source_target_pairs={{0,4},{4,8},{8,12},{12,16},{16,20},{20,24},{24,28},{1,5},{5,9},{9,... | collective-permute-start | bytes 1032200
  209.6 3.0 collective-permute-start.1
  286.6 8.4 %copy-start.3 = (f32[192,2]{0,1:T(2,128)S(1)}, f32[192,2]{0,1:T(2,128)}, u32[]{:S(2)}) copy-start(f32[192,2]{0,1:T(2,128)} %param.9) | copy-start | bytes 4612
  294.7 127.0 %reduce-scatter.5.cloned.1.call-start = ((), (), s32[]{:S(2)}) async-start(), calls=%async_computation.4 | async-start | bytes 3932160 | tf_op jit(solution)/shard_map/reduce_scatter | solution.py:47
  337.8 5.9 %copy-start.1 = (bf16[192,1792]{1,0:T(8,128)(2,1)S(1)}, bf16[192,1792]{1,0:T(8,128)(2,1)}, u32[]{:S(2)}) copy-start(bf16[192,1792]{1,0:T(8,128)(2,1)} %all-reduce.4.cloned.1.call-done) | copy-start | bytes 2064388
Sparse Core Ops, SparseCore 0:
  23.5 58.1 all-reduce.3
  294.8 29.9 all-gather.2
  361.3 60.3 reduce-scatter.4
where the time goes:
time: 429 us; the launch traced here: 428 us
  waiting for transfers between devices  151 us (35%)
  blocking collectives  119 us (28%)
  local copies, waits for them, and re-layouts  64 us (15%)
  other arithmetic  51.5 us (12%)
  matrix products  25 us (6%)
  between operations  14 us (3%)
    reduce_scatter x1, waiting for transfers between devices, per_device(): lax.psum_scatter(lax.dot_general(residual, embed_table, (((1,), (1,)), ((...  60.6 us
    unnamed x1, blocking collectives  58.3 us
    psum x1, waiting for transfers between devices, per_device(): embedded = lax.psum(lookup_rows.astype(jnp.bfloat16), ('pipe', 'vocab'))  55.8 us
    all_to_all x1, blocking collectives, per_device(): lax.all_to_all(buffer, 'expert', split_axis=0, concat_axis=2, tiled=True)[0]  51.2 us
    unnamed x2, other arithmetic  39.8 us
    all_gather x1, waiting for transfers between devices, per_device(): lax.all_gather(shared.astype(jnp.bfloat16), ('pipe', 'vocab'), axis=1, ti...  29.7 us
    dot_general x1, matrix products, per_device(): lax.dot_general(residual, embed_table, (((1,), (1,)), ((), ())), preferre...  17.4 us
    unnamed x20, local copies, waits for them, and re-layouts  16.9 us
  transfers between devices with their start and end apart: 5, of which 4 were waited for; matrix products, arithmetic and copies ran while one was open for 1% of the time, Pallas kernels for 0%

commit v1 on v0

--- a/solution.py
+++ b/solution.py
@@ -36,8 +36,8 @@
     shared = lax.all_to_all(
         shared.astype(jnp.bfloat16), "expert", split_axis=2, concat_axis=0, tiled=True
     ).astype(shared.dtype)
-    returned = lax.all_gather(
-        shared.astype(jnp.bfloat16), ("pipe", "vocab"), axis=1, tiled=True
+    returned = jnp.concatenate(
+        lax.all_gather(shared.astype(jnp.bfloat16), ("pipe", "vocab")), axis=1
     ).astype(shared.dtype)
     picked = returned.reshape(experts * capacity, width_cols)[slot_dest].reshape(
         tokens, top_count, width_cols

time: 429 us -> 458 us (1.068); the launches traced: 428 us -> 450 us
  local copies, waits for them, and re-layouts: 64 us -> 79.9 us
    convert_element_type x0 -> x3, local copies, waits for them, and re-layouts: none -> 17.5 us  [per_device(): returned = jnp.concatenate(lax.all_gather(shared.astype(jnp.bfloat16), ('...]
where the time goes in v1:
time: 458 us; the launch traced here: 450 us
  waiting for transfers between devices  153 us (33%)
  blocking collectives  120 us (26%)
  local copies, waits for them, and re-layouts  79.9 us (17%)
  other arithmetic  53.3 us (12%)
  matrix products  25.2 us (6%)
  between operations  14.3 us (3%)
    reduce_scatter x1, waiting for transfers between devices, per_device(): lax.psum_scatter(lax.dot_general(residual, embed_table, (((1,), (1,)), ((...  60.6 us
    unnamed x1, blocking collectives  58.3 us
    psum x1, waiting for transfers between devices, per_device(): embedded = lax.psum(lookup_rows.astype(jnp.bfloat16), ('pipe', 'vocab'))  55.8 us
    all_to_all x1, blocking collectives, per_device(): lax.all_to_all(buffer, 'expert', split_axis=0, concat_axis=2, tiled=True)[0]  51.6 us
    unnamed x2, other arithmetic  39.8 us
    all_gather x1, waiting for transfers between devices, per_device(): lax.all_gather(shared.astype(jnp.bfloat16), ('pipe', 'vocab'))  32.6 us
    dot_general x1, matrix products, per_device(): lax.dot_general(residual, embed_table, (((1,), (1,)), ((), ())), preferre...  17.6 us
    convert_element_type x3, local copies, waits for them, and re-layouts, per_device(): returned = jnp.concatenate(lax.all_gather(shared.astype(jnp.bfloat16), ('...  17.5 us
  transfers between devices with their start and end apart: 5, of which 4 were waited for; matrix products, arithmetic and copies ran while one was open for 1% of the time, Pallas kernels for 0%

profile of v1, /device:TPU:0, one launch (start us, length us, event | category | flops | bytes accessed | tf_op | source)
XLA Modules:
  0.0 449.7 jit_solution(6012752432301147784)
XLA Ops:
  7.2 14.9 %gather_fusion = bf16[192,1792]{1,0:T(8,128)(2,1)S(1)} fusion(bf16[8192,1792]{1,0:T(8,128)(2,1)} %param.10, s32[1024]{0:T(1024)S(1)} %pad_clamp_fusion.1), kind=kCustom, calls=%fused_computation | custom fusion | bytes 1377024 | tf_op jit(solution)/shard_map/jit(_take)/gather | solution.py:16
  22.1 1.2 select_convert_fusion
  23.8 1.2 reduce-window.6
  25.9 55.8 %all-reduce.4.cloned.1.call-done = bf16[192,1792]{1,0:T(8,128)(2,1)} async-done(((bf16[192,1792]{1,0:T(8,128)(2,1)}), bf16[192,1792]{1,0:T(8,128)(2,1)}) %all-reduce.4.cloned.1.call-update) | async-done | bytes 688144 | tf_op jit(solution)/shard_map/psum | solution.py:18
  81.6 1.8 broadcast_in_dim.42
  84.0 3.3 scatter_custom_fusion
  87.3 51.6 %all_to_all.30 = bf16[4,144,1792]{2,1,0:T(8,128)(2,1)S(1)} all-to-all(bf16[4,144,1792]{2,1,0:T(8,128)(2,1)S(1)} %bitcast.67), channel_id=1, replica_groups=mesh['pipe'=4,'vocab'=2,'expert'=4] {'expert'}, dimensions={0} | all-to-all | bytes 4128768 | tf_op jit(solution)/shard_map/all_to_all | solution.py:28
  138.9 1.1 copy.42
  140.3 1.8 copy-done
  142.1 0.8 fusion.5
  142.8 6.9 %fusion.1 = bf16[1,144,7168]{2,1,0:T(8,128)(2,1)} fusion(bf16[1,256,7168]{2,1,0:T(8,128)(2,1)} %param.13, bf16[144,7168]{1,0:T(8,128)(2,1)S(1)} %bitcast.63, bf16[1,7168,256]{2,1,0:T(8,128)(2,1)} %param.12, f32[144,256]{1,0:T(8,128)S(1)} %fusion.5), kind=kOutput, calls=%fused_computation.5 | convolution fusion | flops 1058217984 | bytes 11616256 | tf_op jit(solution)/shard_map/dot_general | solution.py:32
  149.7 58.3 %fusion = bf16[24,7168]{1,0:T(8,128)(2,1)S(1)} fusion(bf16[1,144,7168]{2,1,0:T(8,128)(2,1)} %fusion.1), kind=kCustom, calls=%all-reduce-scatter | all-reduce-scatter fusion | flops 1376257 | bytes 2408960
  208.0 2.0 collective-permute-start
  210.1 1.7 collective-permute-start.1
  213.0 4.5 collective-permute-done
  217.5 4.8 %concatenate = bf16[66,7168]{1,0:T(8,128)(2,1)S(1)} concatenate(bf16[18,7168]{1,0:T(8,128)(2,1)S(1)} %collective-permute-done.1, bf16[24,7168]{1,0:T(8,128)(2,1)S(1)} %collective-permute-done, bf16[24,7168]{1,0:T(8,128)(2,1)S(1)} %fusion), dimensions={0} | concatenate | bytes 1892352
  222.4 6.0 %copy.43 = bf16[1,18,7168]{1,0,2:T(2,128)(2,1)} copy(bf16[1,18,7168]{2,1,0:T(8,128)(2,1)S(1)} %dynamic-slice_bitcast_fusion) | data formatting | bytes 516096 | tf_op jit(solution)/shard_map/reduce_scatter | solution.py:33
  229.0 39.8 %reduce.4 = bf16[7168,18]{1,0:T(8,128)(2,1)S(1)} reduce(bf16[7168,1,18]{2,1,0:T(2,128)(2,1)} %bitcast.65, bf16[]{:T(256)} %broadcast.68), dimensions={1}, to_apply=%bitcast.56.reduce_sub_computation | reduce | bytes 516098
  268.8 3.4 reshape.110
  272.1 9.7 %all_to_all.31 = bf16[4,2,16128]{2,1,0:T(2,128)(2,1)S(1)} all-to-all(bf16[4,2,16128]{2,1,0:T(2,128)(2,1)S(1)} %reshape.110), channel_id=1, replica_groups=mesh['pipe'=4,'vocab'=2,'expert'=4] {'expert'}, dimensions={0} | all-to-all | bytes 516096 | tf_op jit(solution)/shard_map/all_to_all | solution.py:36
  281.9 5.2 %reshape.111 = bf16[7168,1,18]{2,1,0:T(2,128)(2,1)} reshape(bf16[4,2,16128]{2,1,0:T(2,128)(2,1)S(1)} %all_to_all.31) | data formatting | bytes 516096
  287.1 7.3 %copy.44 = bf16[1,18,7168]{2,1,0:T(8,128)(2,1)S(1)} copy(bf16[1,18,7168]{1,0,2:T(2,128)(2,1)} %bitcast.66) | data formatting | bytes 516096 | tf_op jit(solution)/shard_map/all_to_all | solution.py:36
  295.6 32.6 %all-gather.3.cloned.1.call-done = bf16[32,1,18,1792]{3,2,1,0:T(8,128)(2,1)} async-done(((bf16[4,1,18,1792]{3,2,1,0:T(8,128)(2,1)}), bf16[32,1,18,1792]{3,2,1,0:T(8,128)(2,1)}) %all-gather.3.cloned.1.call-update) | async-done | bytes 2064400 | tf_op jit(solution)/shard_map/all_gather | solution.py:40
  328.3 4.2 copy_convert_fusion
  332.4 5.3 %reshape.101 = f32[8,4,18,1792]{3,1,0,2:T(4,128)} reshape(f32[32,1,18,1792]{3,0,2,1:T(8,128)} %copy_convert_fusion) | data formatting | bytes 8257536 | tf_op jit(solution)/shard_map/convert_element_type | solution.py:41
  337.8 7.0 %copy.47 = f32[4,8,18,1792]{3,2,1,0:T(8,128)} copy(f32[4,8,18,1792]{3,0,1,2:T(4,128)} %bitcast.64) | data formatting | bytes 8257536 | tf_op jit(solution)/shard_map/convert_element_type | solution.py:41
  344.8 5.2 %reshape.75 = f32[576,1792]{1,0:T(8,128)} reshape(f32[4,8,18,1792]{3,2,1,0:T(8,128)} %copy.47) | data formatting | bytes 8257536 | tf_op jit(solution)/shard_map/convert_element_type | solution.py:41
  350.0 6.1 %gather_fusion.1 = f32[384,1792]{1,0:T(8,128)S(1)} fusion(f32[576,1792]{1,0:T(8,128)} %reshape.75, s32[1024]{0:T(1024)S(1)} %pad_clamp_fusion), kind=kCustom, calls=%fused_computation.1 | custom fusion | bytes 5506560 | tf_op jit(solution)/shard_map/gather | solution.py:42
  356.1 2.8 reshape.74
  358.9 5.9 %multiply_reduce_fusion = f32[192,1792]{1,0:T(8,128)S(1)} fusion(f32[192,2,1792]{2,1,0:T(2,128)} %reshape.74, f32[192,2]{1,0:T(8,128)S(1)} %copy.48), kind=kLoop, calls=%fused_computation.11 | loop fusion | flops 1032192 | bytes 4130304 | tf_op jit(solution)/shard_map/reduce_sum | solution.py:45
  364.8 17.6 %convolution_convert_fusion = bf16[192,8192]{1,0:T(8,128)(2,1)} fusion(bf16[8192,1792]{1,0:T(8,128)(2,1)} %param.10, f32[192,1792]{1,0:T(8,128)S(1)} %multiply_reduce_fusion, bf16[192,1792]{1,0:T(8,128)(2,1)S(1)} %copy-done.1), kind=kOutput, calls=%fused_computation.3 | convolution fusion | flops 5639749632 | bytes 34570240 | tf_op jit(solution)/shard_map/dot_general | solution.py:48
  382.4 60.6 %reduce-scatter.5.cloned.1.call-done = bf16[48,8192]{1,0:T(8,128)(2,1)} async-done(((bf16[192,8192]{1,0:T(8,128)(2,1)}), bf16[48,8192]{1,0:T(8,128)(2,1)}) %reduce-scatter.5.cloned.1.call-update) | async-done | bytes 786448 | tf_op jit(solution)/shard_map/reduce_scatter | solution.py:47
  (40 shorter events, 5.3 us)
Async XLA Ops:
  6.5 75.1 %all-reduce.4.cloned.1.call-start = ((), (), s32[]{:S(2)}) async-start(), calls=%async_computation.3 | async-start | bytes 1376256 | tf_op jit(solution)/shard_map/psum | solution.py:18
  7.2 16.2 %copy-start.2 = (s32[192,2]{0,1:T(2,128)S(1)}, s32[192,2]{0,1:T(2,128)}, u32[]{:S(2)}) copy-start(s32[192,2]{0,1:T(2,128)} %param.8) | copy-start | bytes 4612
  23.4 304.9 %all-gather.3.cloned.1.call-start = ((), (), s32[]{:S(2)}) async-start(), calls=%async_computation.5 | async-start | bytes 3096576 | tf_op jit(solution)/shard_map/all_gather | solution.py:40
  140.0 2.0 copy-start
  149.7 62.1 %copy-start.4 = (u32[32]{0:T(128)S(1)}, u32[32]{0:T(128)}, u32[]{:S(2)}) copy-start(u32[32]{0:T(128)} %constant.54) | copy-start | bytes 388
  208.0 9.5 %collective-permute-start = (bf16[24,7168]{1,0:T(8,128)(2,1)S(1)}, bf16[24,7168]{1,0:T(8,128)(2,1)S(1)}, u32[]{:S(2)}, u32[]{:S(2)}) collective-permute-start(bf16[24,7168]{1,0:T(8,128)(2,1)S(1)} %fusion), channel_id=1, source_target_pairs={{0,4},{4,8},{8,12},{12,16},{16,20},{20,24},{24,28},{1,5},{5,9},{9,... | collective-permute-start | bytes 1032200
  210.1 3.0 collective-permute-start.1
  287.1 8.4 %copy-start.3 = (f32[192,2]{0,1:T(2,128)S(1)}, f32[192,2]{0,1:T(2,128)}, u32[]{:S(2)}) copy-start(f32[192,2]{0,1:T(2,128)} %param.9) | copy-start | bytes 4612
  295.3 147.7 %reduce-scatter.5.cloned.1.call-start = ((), (), s32[]{:S(2)}) async-start(), calls=%async_computation.4 | async-start | bytes 3932160 | tf_op jit(solution)/shard_map/reduce_scatter | solution.py:47
  358.9 5.9 %copy-start.1 = (bf16[192,1792]{1,0:T(8,128)(2,1)S(1)}, bf16[192,1792]{1,0:T(8,128)(2,1)}, u32[]{:S(2)}) copy-start(bf16[192,1792]{1,0:T(8,128)(2,1)} %all-reduce.4.cloned.1.call-done) | copy-start | bytes 2064388
Sparse Core Ops, SparseCore 0:
  23.5 58.1 all-reduce.3
  295.4 32.8 all-gather.2
  382.5 60.3 reduce-scatter.4
